TPU v7x, 32 devices: a whole 2x2x4 slice. The times are simulated.
32 devices in a mesh: wave: 16 (over z, y, core), lev: 2 (over x).
Axes of the slice: x: 2, y: 2, z: 4, core: 2. Of those that a mesh axis runs over, the one named last changes fastest.
Arguments:
- control: bfloat16 [2, 256, 256, 2, 512], P(None, 'wave', 'lev'), may hold values from -6 to 6
- wave_of_slot: int32 [256], replicated, may hold values from 0 to 255, each once
- legendre: bfloat16 [256, 256, 256], P('wave', 'lev'), may hold values from -0.375 to 0.375
- vertical: bfloat16 [4, 4, 128, 128], replicated, may hold values from -0.5 to 0.5
- points: int32 [256], P('wave'), may hold values from 128 to 512
- lat_band: int32 [256], P('wave'), may hold values from 0 to 7, never falling along the last dimension, each value on 1 to 64 neighbouring positions
- grid_scale: float32 [8, 512], P(None, 'lev'), may hold values from 0.5 to 2
- obs_weight: bfloat16 [256, 512, 512], P('wave', 'lev'), may hold values from 0.19921875 to 1
Outputs:
- increment: bfloat16 [2, 256, 512, 512], P(None, 'wave', 'lev')
- gradient: bfloat16 [2, 256, 256, 2, 512], P(None, 'wave', 'lev')
Inputs may be any that keep to these rules, and one draw needn't show every extreme that they name: `wave_of_slot`: each zonal wavenumber 0 to 255 stands in exactly one slot. `lat_band`: band numbers never fall from one latitude to the next, and each band covers 1 to 64 latitudes.
All inputs are finite; a program needn't handle non-finite values.
Results may differ from a plain program's by a relative error of at most 0.007.
Values may be sent and summed in bfloat16 or wider, within the bound.
A program may use at most 192 MiB of HBM per device.

v0:
```python
import math
import jax
import jax.numpy as jnp
from jax import lax
from jax.sharding import PartitionSpec as P

WAVES = 256
LONGITUDES = 512
LEVELS = 128
VARIABLES = 4
COV_BANDS = 4


def fourier_table(wave_ids, lat_points):
    lon_index = jnp.arange(LONGITUDES, dtype=jnp.int32)
    remainder = wave_ids[None, :, None] * lon_index[None, None, :] % lat_points[:, None, None]
    angles = (
        2.0
        * math.pi
        * remainder.astype(jnp.float32)
        / lat_points.astype(jnp.float32)[:, None, None]
    )
    factor = jnp.where(wave_ids == 0, 1.0, 2.0).astype(jnp.float32) / math.sqrt(4.0 * WAVES)
    inside = lon_index[None, None, :] < lat_points[:, None, None]
    cosine = jnp.where(inside, factor[None, :, None] * jnp.cos(angles), 0.0)
    sine = jnp.where(inside, -factor[None, :, None] * jnp.sin(angles), 0.0)
    return jnp.stack([cosine, sine], axis=2).astype(jnp.bfloat16)


def vertical_apply(field, vertical, live_rows, band_of, forward):
    members, slots, rows_dev = (field.shape[0], field.shape[1], field.shape[2])
    shaped = field.reshape(members, slots, rows_dev, 2, VARIABLES, LEVELS)
    form = "eskpam,alm->eskpal" if forward else "eskpal,alm->eskpam"
    summed = jnp.zeros(shaped.shape, jnp.float32)
    for index_band in range(COV_BANDS):
        partial_value = jnp.einsum(
            form, shaped, vertical[index_band], preferred_element_type=jnp.float32
        )
        chosen = live_rows & (band_of == index_band)
        summed = summed + jnp.where(chosen[None, :, :, None, None, None], partial_value, 0.0)
    return summed.reshape(field.shape).astype(jnp.bfloat16)


def to_bands(values):
    return lax.all_to_all(values, "wave", split_axis=2, concat_axis=1, tiled=True)


def shards(control, wave_of_slot, legendre, vertical, points, lat_band, grid_scale, obs_weight):
    members, slots, rows_dev = (control.shape[0], control.shape[1], control.shape[2])
    slot_start = lax.axis_index("wave") * slots
    row_start = lax.axis_index("lev") * rows_dev
    own_waves = lax.dynamic_slice_in_dim(wave_of_slot, slot_start, slots)
    row_index = row_start + jnp.arange(rows_dev, dtype=jnp.int32)
    totals_n = own_waves[:, None] + row_index[None, :]
    live_rows = totals_n <= WAVES - 1
    band_of = jnp.minimum(totals_n * COV_BANDS // WAVES, COV_BANDS - 1)
    spectral = vertical_apply(control, vertical, live_rows, band_of, True)
    columns = lax.all_to_all(spectral, "lev", split_axis=4, concat_axis=2, tiled=True)
    col_dev = columns.shape[4]
    width = 2 * col_dev
    all_rows = columns.shape[2]
    columns = columns.reshape(members, slots, all_rows, width)
    coeffs = jnp.einsum(
        "skt,eskq->estq",
        lax.all_gather(legendre, "lev", axis=1, tiled=True),
        columns,
        preferred_element_type=jnp.float32,
    )
    coeffs = coeffs.astype(jnp.bfloat16)
    by_lat = to_bands(coeffs)
    wave_count = by_lat.shape[1]
    lat_dev = by_lat.shape[2]
    by_lat = by_lat.reshape(members, wave_count, lat_dev, 2, col_dev)
    fourier = fourier_table(wave_of_slot, points)
    synthesis = jnp.einsum("tspj,estpc->etcj", fourier, by_lat, preferred_element_type=jnp.float32)
    chooser = (
        lat_band[:, None] == jnp.arange(grid_scale.shape[0], dtype=jnp.int32)[None, :]
    ).astype(jnp.float32)
    lat_scale = jnp.dot(chooser, grid_scale, precision=lax.Precision.HIGHEST)
    increment = (synthesis * lat_scale[None, :, :, None]).astype(jnp.bfloat16)
    weighted = (
        increment.astype(jnp.float32) * obs_weight.astype(jnp.float32) * lat_scale[None, :, :, None]
    ).astype(jnp.bfloat16)
    adjoint_fourier = jnp.einsum(
        "tspj,etcj->etspc", fourier, weighted, preferred_element_type=jnp.float32
    )
    adjoint_fourier = adjoint_fourier.astype(jnp.bfloat16).reshape(
        members, lat_dev, wave_count, width
    )
    band_rows = to_bands(adjoint_fourier)
    adjoint_coeffs = jnp.einsum(
        "skt,etsq->eskq",
        lax.all_gather(legendre, "lev", axis=1, tiled=True),
        band_rows,
        preferred_element_type=jnp.float32,
    )
    adjoint_coeffs = adjoint_coeffs.astype(jnp.bfloat16).reshape(
        members, slots, all_rows, 2, col_dev
    )
    rows_back = lax.all_to_all(adjoint_coeffs, "lev", split_axis=2, concat_axis=4, tiled=True)
    gradient = vertical_apply(rows_back, vertical, live_rows, band_of, False)
    return (increment, gradient)


def solution(mesh):
    in_specs = (
        P(None, "wave", "lev", None, None),
        P(),
        P("wave", "lev", None),
        P(),
        P("wave"),
        P("wave"),
        P(None, "lev"),
        P("wave", "lev", None),
    )
    out_specs = (P(None, "wave", "lev", None), P(None, "wave", "lev", None, None))
    return jax.shard_map(shards, mesh=mesh, in_specs=in_specs, out_specs=out_specs, check_vma=False)
```

profile of v0, /device:TPU:0, one launch (start us, length us, event | category | flops | bytes accessed | tf_op | source)
XLA Modules:
  0.0 1023.2 jit_solution(5257670310123423608)
XLA Ops:
  7.2 0.0 copy-start
  7.2 0.0 copy-start.4
  7.2 14.1 %reshape.273 = bf16[2,16,128,2,4,128]{5,4,3,2,1,0:T(4,128)(2,1)} reshape(bf16[2,16,128,2,512]{4,3,2,1,0:T(2,128)(2,1)} %param.8) | data formatting | bytes 16777216 | tf_op jit(solution)/shard_map/reshape | solution.py:32
  21.3 0.0 copy-done.4
  21.3 11.6 %fusion.28 = f32[4,128,2,16,128,2]{4,1,5,3,2,0:T(8,128)} fusion(bf16[2,16,128,2,4,128]{5,4,3,2,1,0:T(4,128)(2,1)} %reshape.273, bf16[4,4,128,128]{3,2,1,0:T(8,128)(2,1)S(1)} %copy-done.4), kind=kOutput, calls=%fused_computation.35 | convolution fusion | flops 1073741824 | bytes 25296896 | tf_op jit(solution)/shard_map/eskpam,alm->eskpal/dot_general | solution.py:36
  32.9 0.0 copy-done.2
  32.9 8.1 fusion.30
  41.0 8.1 fusion.32
  49.1 0.0 copy-done.13
  49.1 0.1 dynamic_slice.3
  49.2 0.1 fusion.68
  49.3 0.0 copy-start.5
  49.3 0.0 copy-start.7
  49.3 0.6 copy-done.5
  49.8 0.0 copy-done.7
  49.9 0.0 copy-done.11
  49.9 23.9 %fusion.34 = bf16[2,16,128,2,4,128]{2,5,3,1,0,4:T(8,128)(2,1)} fusion(bf16[2,16,128,2,4,128]{5,4,3,2,1,0:T(4,128)(2,1)} %reshape.273, pred[16,128]{1,0:T(8,128)(4,1)S(1)} %get-tuple-element.14, f32[4,128,2,16,128,2]{4,1,5,3,2,0:T(8,128)} %fusion.28, pred[16,128]{1,0:T(8,128)(4,1)S(1)} %get-tuple-element.15, f32[4,128,2,16,128,2]{4,1,5,3,2,0:T(8,128)} %fusion.30, ...), kind=kOutput, calls=%fused_computation.41 | convolution fusion | flops 1107296256 | bytes 67248128 | tf_op jit(solution)/shard_map/eskpam,alm->eskpal/dot_general | solution.py:36
  73.8 10.5 %copy.73 = bf16[2,16,128,2,4,128]{2,5,4,3,1,0:T(8,128)(2,1)} copy(bf16[2,16,128,2,4,128]{2,5,3,1,0,4:T(8,128)(2,1)} %fusion.34) | data formatting | bytes 16777216 | tf_op jit(solution)/shard_map/add | solution.py:40
  84.3 13.1 %copy.74 = bf16[2,16,128,2,512]{2,3,1,0,4:T(2,128)(2,1)} copy(bf16[2,16,128,2,512]{2,4,3,1,0:T(8,128)(2,1)} %bitcast.123) | data formatting | bytes 16777216 | tf_op jit(solution)/shard_map/convert_element_type | solution.py:41
  97.5 6.9 all-to-all-start
  104.4 0.0 all-gather.2.cloned.1.call-start
  104.5 0.7 all-gather.2.cloned.1.call-update
  105.1 115.7 %all-to-all-done = bf16[2,16,128,2,512]{2,3,1,0,4:T(2,128)(2,1)} async-done(((bf16[2,16,128,2,512]{2,3,1,0,4:T(2,128)(2,1)}), bf16[2,16,128,2,512]{2,3,1,0,4:T(2,128)(2,1)}, u32[]{:S(2)}, u32[]{:S(2)}) %all-to-all-start) | async-done | bytes 8388640 | tf_op jit(solution)/shard_map/all_to_all | solution.py:58
  220.8 16.5 %copy.75 = bf16[2,16,128,2,512]{2,4,3,1,0:T(8,128)(2,1)} copy(bf16[2,16,128,2,512]{2,3,1,0,4:T(2,128)(2,1)} %all-to-all-done) | data formatting | bytes 16777216 | tf_op jit(solution)/shard_map/all_to_all | solution.py:58
  237.3 16.8 %copy.76 = bf16[2,16,2,128,2,256]{3,2,5,4,0,1:T(2,128)(2,1)} copy(bf16[2,16,2,128,2,256]{3,5,2,4,1,0:T(8,128)(2,1)} %bitcast.124) | data formatting | bytes 16777216 | tf_op jit(solution)/shard_map/all_to_all | solution.py:58
  254.0 14.0 %reshape.274 = bf16[2,16,256,512]{2,3,0,1:T(8,128)(2,1)} reshape(bf16[2,16,2,128,2,256]{3,2,5,4,0,1:T(2,128)(2,1)} %copy.76) | data formatting | bytes 16777216 | tf_op jit(solution)/shard_map/reshape | solution.py:62
  268.1 9.7 convert_bitcast_fusion
  277.8 21.1 %copy.77 = bf16[2,16,256,512]{3,0,1,2:T(2,128)(2,1)} copy(bf16[2,16,256,512]{2,3,0,1:T(8,128)(2,1)} %convert_bitcast_fusion) | data formatting | bytes 16777216 | tf_op jit(solution)/shard_map/convert_element_type | solution.py:69
  298.8 6.2 all-to-all-start.1
  305.0 0.0 copy-start.14
  305.0 0.0 copy-start.15
  305.0 6.6 convert_element_type.68
  311.6 0.0 copy-done.14
  311.6 0.1 iota_compare_fusion
  311.7 0.0 copy-done.15
  311.7 0.2 fusion.73
  311.9 0.1 iota_multiply_fusion
  312.0 121.6 %select_convert_fusion.1 = (bf16[16,256,1,512]{3,1,2,0:T(8,128)(2,1)}, bf16[16,256,1,512]{3,1,2,0:T(8,128)(2,1)}) fusion(f32[256]{0:T(256)S(1)} %get-tuple-element.16, f32[16]{0:T(128)S(1)} %get-tuple-element.19, pred[16]{0:T(512)(128)(4,1)S(1)} %broadcast_compare_fusion, s32[16]{0:T(128)S(1)} %get-tuple-element.18, s32[256,512]{1,0:T(8,128)S(1)} %iota_multiply_fusion, ...), kind=kLoop, calls=%fused_computation.21 | loop fusion | flops 33554432 | bytes 8923280 | tf_op jit(solution)/shard_map/convert.1
  433.6 21.9 %all-to-all-done.1 = bf16[2,16,256,512]{3,0,1,2:T(2,128)(2,1)} async-done(((bf16[2,16,256,512]{3,0,1,2:T(2,128)(2,1)}), bf16[2,16,256,512]{3,0,1,2:T(2,128)(2,1)}, u32[]{:S(2)}, u32[]{:S(2)}) %all-to-all-start.1) | async-done | bytes 8388640 | tf_op jit(solution)/shard_map/all_to_all | solution.py:45
  455.6 11.5 %copy.78 = bf16[2,16,256,512]{3,2,1,0:T(8,128)(2,1)} copy(bf16[2,16,256,512]{3,0,1,2:T(2,128)(2,1)} %all-to-all-done.1) | data formatting | bytes 16777216 | tf_op jit(solution)/shard_map/all_to_all | solution.py:45
  467.1 8.2 copy.79
  475.3 12.5 %reshape.275 = bf16[2,256,16,2,256]{4,3,2,1,0:T(2,128)(2,1)} reshape(bf16[2,16,16,16,512]{4,3,2,1,0:T(8,128)(2,1)} %copy.79) | data formatting | bytes 16777216 | tf_op jit(solution)/shard_map/reshape | solution.py:73
  487.8 17.3 %fusion.40 = bf16[2,16,256,512]{3,2,0,1:T(8,128)(2,1)} fusion(f32[16,256]{1,0:T(8,128)S(1)} %fusion.73, bf16[16,256,1,512]{3,1,2,0:T(8,128)(2,1)} %get-tuple-element.11, bf16[16,256,1,512]{3,1,2,0:T(8,128)(2,1)} %get-tuple-element.10, bf16[2,256,16,2,256]{4,3,2,1,0:T(2,128)(2,1)} %reshape.275), kind=kOutput, calls=%fused_computation.43 | convolution fusion | flops 4307550208 | bytes 25182208 | tf_op jit(solution)/shard_map/tspj,estpc->etcj/dot_general | solution.py:75
  505.0 13.4 %fusion.17 = bf16[16,2,256,256,2]{3,2,4,1,0:T(8,128)(2,1)} fusion(bf16[2,16,256,512]{3,2,0,1:T(8,128)(2,1)} %fusion.40, f32[16,256]{1,0:T(8,128)S(1)} %fusion.73, f32[16,256,512]{2,1,0:T(8,128)} %convert_element_type.68, bf16[16,256,1,512]{3,1,2,0:T(8,128)(2,1)} %get-tuple-element.11, bf16[16,256,1,512]{3,1,2,0:T(8,128)(2,1)} %get-tuple-element.10), kind=kOutput, calls=%fused_computation.26 | convolution fusion | flops 4332716032 | bytes 33570816 | tf_op jit(solution)/shard_map/tspj,etcj->etspc/dot_general | solution.py:84
  518.5 14.6 %copy.81 = bf16[2,16,256,512]{3,1,0,2:T(8,128)(2,1)} copy(bf16[2,16,256,512]{2,3,0,1:T(8,128)(2,1)} %bitcast.129) | data formatting | bytes 16777216 | tf_op jit(solution)/shard_map/reshape | solution.py:87
  533.0 218.6 %all_to_all.63 = bf16[2,16,256,512]{3,1,0,2:T(8,128)(2,1)} all-to-all(bf16[2,16,256,512]{3,1,0,2:T(8,128)(2,1)} %copy.81), channel_id=1, replica_groups=mesh['wave'=16,'lev'=2] {'wave'}, dimensions={2} | all-to-all | bytes 16777216 | tf_op jit(solution)/shard_map/all_to_all | solution.py:45
  751.6 15.5 %copy.83 = bf16[2,16,16,16,512]{4,3,2,1,0:T(8,128)(2,1)} copy(bf16[2,16,16,16,512]{4,2,0,3,1:T(8,128)(2,1)} %bitcast.126) | data formatting | bytes 16777216 | tf_op jit(solution)/shard_map/all_to_all | solution.py:45
  767.1 0.0 copy-done.3
  767.1 12.7 %fusion.14 = bf16[16,2,512,256]{3,2,1,0:T(8,128)(2,1)} fusion(bf16[2,256,16,512]{3,2,1,0:T(8,128)(2,1)} %bitcast.121, bf16[16,256,256]{2,1,0:T(8,128)(2,1)S(1)} %copy-done.3), kind=kOutput, calls=%fused_computation.25 | convolution fusion | flops 2151677952 | bytes 18874368 | tf_op jit(solution)/shard_map/skt,etsq->eskq/dot_general | solution.py:91
  779.7 21.1 %copy.85 = bf16[2,16,256,2,256]{4,3,1,0,2:T(2,128)(2,1)} copy(bf16[2,16,256,2,256]{2,4,3,0,1:T(8,128)(2,1)} %bitcast.122) | data formatting | bytes 16777216 | tf_op jit(solution)/shard_map/reshape | solution.py:97
  800.8 7.0 all-to-all-start.3
  807.8 7.7 copy.97
  815.5 86.1 %all-to-all-done.3 = bf16[2,16,256,2,256]{4,3,1,0,2:T(2,128)(2,1)} async-done(((bf16[2,16,256,2,256]{4,3,1,0,2:T(2,128)(2,1)}), bf16[2,16,256,2,256]{4,3,1,0,2:T(2,128)(2,1)}, u32[]{:S(2)}, u32[]{:S(2)}) %all-to-all-start.3) | async-done | bytes 8388640 | tf_op jit(solution)/shard_map/all_to_all | solution.py:100
  901.5 13.6 %copy.86 = bf16[2,16,256,2,256]{4,2,3,1,0:T(8,128)(2,1)} copy(bf16[2,16,256,2,256]{4,3,1,0,2:T(2,128)(2,1)} %all-to-all-done.3) | data formatting | bytes 16777216 | tf_op jit(solution)/shard_map/all_to_all | solution.py:100
  915.2 12.1 %copy.87 = bf16[2,16,128,2,2,256]{2,5,4,3,1,0:T(8,128)(2,1)} copy(bf16[2,16,128,2,2,256]{5,2,4,3,1,0:T(8,128)(2,1)} %bitcast.127) | data formatting | bytes 16777216 | tf_op jit(solution)/shard_map/all_to_all | solution.py:100
  927.3 11.5 %fusion.21 = f32[4,2,16,128,2,128]{3,5,4,2,1,0:T(8,128)} fusion(bf16[2,16,128,2,4,128]{2,5,4,3,1,0:T(8,128)(2,1)} %bitcast.117, bf16[4,4,128,128]{3,2,1,0:T(8,128)(2,1)S(1)} %copy-done.4), kind=kOutput, calls=%fused_computation.28 | convolution fusion | flops 1073741824 | bytes 25296896 | tf_op jit(solution)/shard_map/eskpal,alm->eskpam/dot_general | solution.py:36
  938.7 11.5 %fusion.23 = f32[4,2,16,128,2,128]{3,5,4,2,1,0:T(8,128)} fusion(bf16[2,16,128,2,4,128]{2,5,4,3,1,0:T(8,128)(2,1)} %bitcast.118, bf16[4,4,128,128]{3,2,1,0:T(8,128)(2,1)S(1)} %copy-done.4), kind=kOutput, calls=%fused_computation.30 | convolution fusion | flops 1073741824 | bytes 25296896 | tf_op jit(solution)/shard_map/eskpal,alm->eskpam/dot_general | solution.py:36
  950.2 11.5 %fusion.25 = f32[4,2,16,128,2,128]{3,5,4,2,1,0:T(8,128)} fusion(bf16[2,16,128,2,4,128]{2,5,4,3,1,0:T(8,128)(2,1)} %bitcast.119, bf16[4,4,128,128]{3,2,1,0:T(8,128)(2,1)S(1)} %copy-done.4), kind=kOutput, calls=%fused_computation.32 | convolution fusion | flops 1073741824 | bytes 25296896 | tf_op jit(solution)/shard_map/eskpal,alm->eskpam/dot_general | solution.py:36
  961.7 0.0 copy-done.6
  961.7 0.0 copy-done.10
  961.7 23.0 %fusion.37 = bf16[2,16,128,2,4,128]{2,5,3,1,0,4:T(8,128)(2,1)} fusion(bf16[2,16,128,2,4,128]{2,5,4,3,1,0:T(8,128)(2,1)} %bitcast.120, pred[16,128]{1,0:T(8,128)(4,1)S(1)} %copy-done.10, f32[4,2,16,128,2,128]{3,5,4,2,1,0:T(8,128)} %fusion.21, pred[16,128]{1,0:T(8,128)(4,1)S(1)} %copy-done.12, f32[4,2,16,128,2,128]{3,5,4,2,1,0:T(8,128)} %fusion.23, ...), kind=kOutput, calls=%fused_computation.42 | convolution fusion | flops 1107296256 | bytes 67248128 | tf_op jit(solution)/shard_map/eskpal,alm->eskpam/dot_general | solution.py:36
  984.7 10.4 %copy.96 = bf16[2,16,128,2,4,128]{2,5,4,3,1,0:T(8,128)(2,1)} copy(bf16[2,16,128,2,4,128]{2,5,3,1,0,4:T(8,128)(2,1)} %fusion.37) | data formatting | bytes 16777216 | tf_op jit(solution)/shard_map/add | solution.py:40
  995.1 21.1 %copy.98 = bf16[2,16,128,2,512]{4,3,2,1,0:T(2,128)(2,1)} copy(bf16[2,16,128,2,512]{2,4,3,1,0:T(8,128)(2,1)} %bitcast.128) | data formatting | bytes 16777216
  1016.2 0.0 copy-done.1
  (19 shorter events, 0.0 us)
Async XLA Ops:
  7.2 304.5 %copy-start = (f32[8,256]{1,0:T(8,128)S(1)}, f32[8,256]{1,0:T(8,128)}, u32[]{:S(2)}) copy-start(f32[8,256]{1,0:T(8,128)} %param.14) | copy-start | bytes 24580
  7.2 14.1 %copy-start.4 = (bf16[4,4,128,128]{3,2,1,0:T(8,128)(2,1)S(1)}, bf16[4,4,128,128]{3,2,1,0:T(8,128)(2,1)}, u32[]{:S(2)}) copy-start(bf16[4,4,128,128]{3,2,1,0:T(8,128)(2,1)} %param.11) | copy-start | bytes 1572868
  21.3 11.6 %copy-start.2 = (bf16[2,16,128,2,4,128]{5,4,3,2,1,0:T(4,128)(2,1)S(1)}, bf16[2,16,128,2,4,128]{5,4,3,2,1,0:T(4,128)(2,1)}, u32[]{:S(2)}) copy-start(bf16[2,16,128,2,4,128]{5,4,3,2,1,0:T(4,128)(2,1)} %reshape.273) | copy-start | bytes 25165828
  41.0 8.1 copy-start.13
  49.3 0.6 copy-start.5
  49.3 0.6 copy-start.7
  49.3 0.6 copy-start.9
  49.3 0.6 copy-start.11
  97.5 123.3 %all-to-all-start = ((bf16[2,16,128,2,512]{2,3,1,0,4:T(2,128)(2,1)}), bf16[2,16,128,2,512]{2,3,1,0,4:T(2,128)(2,1)}, u32[]{:S(2)}, u32[]{:S(2)}) async-start(bf16[2,16,128,2,512]{2,3,1,0,4:T(2,128)(2,1)} %copy.74), calls=%async_computation | async-start | bytes 16777216 | tf_op jit(solution)/shard_map/all_to_all | solution.py:58
  104.4 163.7 %all-gather.2.cloned.1.call-start = ((), (), s32[]{:S(2)}) async-start(), calls=%async_computation.4 | async-start | bytes 3145728 | tf_op jit(solution)/shard_map/all_gather | solution.py:65
  298.8 156.7 %all-to-all-start.1 = ((bf16[2,16,256,512]{3,0,1,2:T(2,128)(2,1)}), bf16[2,16,256,512]{3,0,1,2:T(2,128)(2,1)}, u32[]{:S(2)}, u32[]{:S(2)}) async-start(bf16[2,16,256,512]{3,0,1,2:T(2,128)(2,1)} %copy.77), calls=%async_computation.1 | async-start | bytes 16777216 | tf_op jit(solution)/shard_map/all_to_all | solution.py:45
  305.0 6.6 copy-start.14
  305.0 6.7 copy-start.15
  751.6 15.5 %copy-start.3 = (bf16[16,256,256]{2,1,0:T(8,128)(2,1)S(1)}, bf16[16,256,256]{2,1,0:T(8,128)(2,1)}, u32[]{:S(2)}) copy-start(bf16[16,256,256]{2,1,0:T(8,128)(2,1)} %all-gather.2.cloned.1.call-done) | copy-start | bytes 6291460
  800.8 100.7 %all-to-all-start.3 = ((bf16[2,16,256,2,256]{4,3,1,0,2:T(2,128)(2,1)}), bf16[2,16,256,2,256]{4,3,1,0,2:T(2,128)(2,1)}, u32[]{:S(2)}, u32[]{:S(2)}) async-start(bf16[2,16,256,2,256]{4,3,1,0,2:T(2,128)(2,1)} %copy.85), calls=%async_computation.3 | async-start | bytes 16777216 | tf_op jit(solution)/shard_map/all_to_all | solution.py:100
  950.2 11.5 %copy-start.6 = (pred[16,128]{1,0:T(8,128)(4,1)S(1)}, pred[16,128]{1,0:T(8,128)(4,1)}, u32[]{:S(2)}) copy-start(pred[16,128]{1,0:T(8,128)(4,1)} %copy-done.5) | copy-start | bytes 6148
  950.2 11.5 %copy-start.8 = (pred[16,128]{1,0:T(8,128)(4,1)S(1)}, pred[16,128]{1,0:T(8,128)(4,1)}, u32[]{:S(2)}) copy-start(pred[16,128]{1,0:T(8,128)(4,1)} %copy-done.7) | copy-start | bytes 6148
  950.2 11.5 %copy-start.10 = (pred[16,128]{1,0:T(8,128)(4,1)S(1)}, pred[16,128]{1,0:T(8,128)(4,1)}, u32[]{:S(2)}) copy-start(pred[16,128]{1,0:T(8,128)(4,1)} %copy-done.9) | copy-start | bytes 6148
  950.2 11.5 %copy-start.12 = (pred[16,128]{1,0:T(8,128)(4,1)S(1)}, pred[16,128]{1,0:T(8,128)(4,1)}, u32[]{:S(2)}) copy-start(pred[16,128]{1,0:T(8,128)(4,1)} %copy-done.11) | copy-start | bytes 6148
  995.1 21.1 %copy-start.1 = (f32[8,256]{1,0:T(8,128)S(1)}, f32[8,256]{1,0:T(8,128)}, u32[]{:S(2)}) copy-start(f32[8,256]{1,0:T(8,128)} %param.14) | copy-start | bytes 24580
Sparse Core Ops, SparseCore 0:
  106.8 58.8 all-gather.1
where the time goes:
time: 1030 us; the launch traced here: 1020 us
  local copies, waits for them, and re-layouts  255 us (25%)
  waiting for transfers between devices  224 us (22%)
  blocking collectives  219 us (21%)
  matrix products  162 us (16%)
  other arithmetic  128 us (12%)
  starting transfers between devices  20.1 us (2%)
  between operations  14.4 us (1%)
    all_to_all x1, blocking collectives, to_bands(): lax.all_to_all(values, 'wave', split_axis=2, concat_axis=1, tiled=True)  219 us
    another operation x1, other arithmetic  122 us
    all_to_all x1, waiting for transfers between devices, shards(): lax.all_to_all(spectral, 'lev', split_axis=4, concat_axis=2, tiled=True)  116 us
    dot_general x8, matrix products, vertical_apply(): jnp.einsum(form, shaped, vertical[index_band], preferred_element_type=jnp...  109 us
    all_to_all x1, waiting for transfers between devices, shards(): lax.all_to_all(adjoint_coeffs, 'lev', split_axis=2, concat_axis=4, tiled=...  86.1 us
    all_to_all x3, local copies, waits for them, and re-layouts, to_bands(): lax.all_to_all(values, 'wave', split_axis=2, concat_axis=1, tiled=True)  35.2 us
    all_to_all x2, local copies, waits for them, and re-layouts, shards(): lax.all_to_all(spectral, 'lev', split_axis=4, concat_axis=2, tiled=True)  33.2 us
    unnamed x34, local copies, waits for them, and re-layouts  29.4 us
  transfers between devices with their start and end apart: 4, of which 3 were waited for; matrix products, arithmetic and copies ran while one was open for 18% of the time, Pallas kernels for 0%

commit v1 on v0

--- a/solution.py
+++ b/solution.py
@@ -9,6 +9,13 @@
 LEVELS = 128
 VARIABLES = 4
 COV_BANDS = 4
+
+
+def exchange_blocks(x, name, split, join):
+    size = lax.axis_size(name)
+    tiles = jnp.stack(jnp.split(x, size, axis=split), axis=0)
+    tiles = lax.all_to_all(tiles, name, split_axis=0, concat_axis=0)
+    return jnp.concatenate(tiles, axis=join)
 
 
 def fourier_table(wave_ids, lat_points):
@@ -42,7 +49,7 @@
 
 
 def to_bands(values):
-    return lax.all_to_all(values, "wave", split_axis=2, concat_axis=1, tiled=True)
+    return exchange_blocks(values, "wave", 2, 1)
 
 
 def shards(control, wave_of_slot, legendre, vertical, points, lat_band, grid_scale, obs_weight):

time: 1030 us -> 1120 us (1.087)
  local copies, waits for them, and re-layouts: 255 us -> 335 us
    unnamed x34 -> x89, local copies, waits for them, and re-layouts: 29.4 us -> 117 us
    split x0 -> x1, local copies, waits for them, and re-layouts: none -> 48.6 us  [exchange_blocks(): tiles = jnp.stack(jnp.split(x, size, axis=split), axis=0)]
    reshape x2 -> x0, local copies, waits for them, and re-layouts: 27 us -> none  [the longest x1 14.6 us: shards(): adjoint_fourier.astype(jnp.bfloat16)]
    all_to_all x3 -> x1, local copies, waits for them, and re-layouts: 35.2 us -> 8.52 us  [exchange_blocks(): tiles = lax.all_to_all(tiles, name, split_axis=0, concat_axis=0)]
    convert_element_type x1 -> x0, local copies, waits for them, and re-layouts: 21.1 us -> none  [shards(): coeffs = coeffs.astype(jnp.bfloat16)]
    another operation x0 -> x3, local copies, waits for them, and re-layouts: none -> 13.3 us  [the longest x1 12.5 us: shards(): by_lat = by_lat.reshape(members, wave_count, lat_dev, 2, col_dev)]
  transfers between devices with their start and end apart: 4 -> 4, of which waited for: 3 -> 3; matrix products, arithmetic and copies ran while one was open for 18% -> 17% of each run, Pallas kernels for 0% -> 0%
where the time goes in v1:
time: 1120 us; the launch traced here: 1110 us
  local copies, waits for them, and re-layouts  335 us (30%)
  waiting for transfers between devices  224 us (20%)
  blocking collectives  219 us (20%)
  matrix products  167 us (15%)
  other arithmetic  127 us (11%)
  starting transfers between devices  20.5 us (2%)
  between operations  14.6 us (1%)
    all_to_all x1, blocking collectives, exchange_blocks(): tiles = lax.all_to_all(tiles, name, split_axis=0, concat_axis=0)  219 us
    another operation x1, other arithmetic  120 us
    unnamed x89, local copies, waits for them, and re-layouts  117 us
    all_to_all x1, waiting for transfers between devices, shards(): lax.all_to_all(spectral, 'lev', split_axis=4, concat_axis=2, tiled=True)  115 us
    dot_general x8, matrix products, vertical_apply(): jnp.einsum(form, shaped, vertical[index_band], preferred_element_type=jnp...  109 us
    all_to_all x1, waiting for transfers between devices, shards(): lax.all_to_all(adjoint_coeffs, 'lev', split_axis=2, concat_axis=4, tiled=...  86.1 us
    split x1, local copies, waits for them, and re-layouts, exchange_blocks(): tiles = jnp.stack(jnp.split(x, size, axis=split), axis=0)  48.6 us
    all_to_all x2, local copies, waits for them, and re-layouts, shards(): lax.all_to_all(spectral, 'lev', split_axis=4, concat_axis=2, tiled=True)  37.6 us
  transfers between devices with their start and end apart: 4, of which 3 were waited for; matrix products, arithmetic and copies ran while one was open for 17% of the time, Pallas kernels for 0%

profile of v1, /device:TPU:0, one launch (start us, length us, event | category | flops | bytes accessed | tf_op | source)
XLA Modules:
  0.0 1107.3 jit_solution(6117608717691415548)
XLA Ops:
  7.2 14.1 %reshape.278 = bf16[2,16,128,2,4,128]{5,4,3,2,1,0:T(4,128)(2,1)} reshape(bf16[2,16,128,2,512]{4,3,2,1,0:T(2,128)(2,1)} %param.8) | data formatting | bytes 16777216 | tf_op jit(solution)/shard_map/reshape | solution.py:39
  21.3 11.6 %fusion.30 = f32[4,128,2,16,128,2]{4,1,5,3,2,0:T(8,128)} fusion(bf16[2,16,128,2,4,128]{5,4,3,2,1,0:T(4,128)(2,1)} %reshape.278, bf16[4,4,128,128]{3,2,1,0:T(8,128)(2,1)S(1)} %copy-done.4), kind=kOutput, calls=%fused_computation.37 | convolution fusion | flops 1073741824 | bytes 25296896 | tf_op jit(solution)/shard_map/eskpam,alm->eskpal/dot_general | solution.py:43
  32.9 8.1 fusion.28
  41.0 8.1 fusion.32
  49.9 23.9 %fusion.34 = bf16[2,16,128,2,4,128]{2,5,3,1,0,4:T(8,128)(2,1)} fusion(bf16[2,16,128,2,4,128]{5,4,3,2,1,0:T(4,128)(2,1)} %reshape.278, pred[16,128]{1,0:T(8,128)(4,1)S(1)} %get-tuple-element.30, f32[4,128,2,16,128,2]{4,1,5,3,2,0:T(8,128)} %fusion.28, pred[16,128]{1,0:T(8,128)(4,1)S(1)} %get-tuple-element.31, f32[4,128,2,16,128,2]{4,1,5,3,2,0:T(8,128)} %fusion.30, ...), kind=kOutput, calls=%fused_computation.41 | convolution fusion | flops 1107296256 | bytes 67248128 | tf_op jit(solution)/shard_map/eskpam,alm->eskpal/dot_general | solution.py:43
  73.8 10.5 copy.103
  84.3 13.1 %copy.104 = bf16[2,16,128,2,512]{2,3,1,0,4:T(2,128)(2,1)} copy(bf16[2,16,128,2,512]{2,4,3,1,0:T(8,128)(2,1)} %bitcast.222) | data formatting | bytes 16777216 | tf_op jit(solution)/shard_map/convert_element_type | solution.py:48
  97.5 7.1 all-to-all-start
  104.6 1.3 copy.107
  106.0 115.0 %all-to-all-done = bf16[2,16,128,2,512]{2,3,1,0,4:T(2,128)(2,1)} async-done(((bf16[2,16,128,2,512]{2,3,1,0,4:T(2,128)(2,1)}), bf16[2,16,128,2,512]{2,3,1,0,4:T(2,128)(2,1)}, u32[]{:S(2)}, u32[]{:S(2)}) %all-to-all-start) | async-done | bytes 8388640 | tf_op jit(solution)/shard_map/all_to_all | solution.py:65
  221.0 16.5 %copy.105 = bf16[2,16,128,2,512]{2,4,3,1,0:T(8,128)(2,1)} copy(bf16[2,16,128,2,512]{2,3,1,0,4:T(2,128)(2,1)} %all-to-all-done) | data formatting | bytes 16777216 | tf_op jit(solution)/shard_map/all_to_all | solution.py:65
  237.4 21.1 %copy.106 = bf16[2,16,2,128,2,256]{5,4,3,2,0,1:T(2,128)(2,1)} copy(bf16[2,16,2,128,2,256]{3,5,2,4,1,0:T(8,128)(2,1)} %bitcast.223) | data formatting | bytes 16777216 | tf_op jit(solution)/shard_map/all_to_all | solution.py:65
  258.5 14.4 %reshape.279 = bf16[2,16,256,512]{3,2,0,1:T(8,128)(2,1)} reshape(bf16[2,16,2,128,2,256]{5,4,3,2,0,1:T(2,128)(2,1)} %copy.106) | data formatting | bytes 16777216 | tf_op jit(solution)/shard_map/reshape | solution.py:69
  273.0 6.4 convert_bitcast_fusion
  279.3 0.8 fusion.60
  281.8 0.8 fusion.57
  282.7 0.8 fusion.56
  292.6 6.2 all-to-all-start.1
  298.8 6.7 convert_element_type.68
  306.0 120.4 %select_convert_fusion.1 = (bf16[16,256,1,512]{3,1,2,0:T(8,128)(2,1)}, bf16[16,256,1,512]{3,1,2,0:T(8,128)(2,1)}) fusion(f32[256]{0:T(256)S(1)} %get-tuple-element.32, f32[16]{0:T(128)S(1)} %get-tuple-element.35, pred[16]{0:T(512)(128)(4,1)S(1)} %broadcast_compare_fusion, s32[16]{0:T(128)S(1)} %get-tuple-element.34, s32[256,512]{1,0:T(8,128)S(1)} %iota_multiply_fusion, ...), kind=kLoop, calls=%fused_computation.21 | loop fusion | flops 33554432 | bytes 8923280 | tf_op jit(solution)/shard_map/convert.1
  426.4 23.0 %all-to-all-done.1 = bf16[16,2,16,16,512]{4,3,1,2,0:T(8,128)(2,1)} async-done(((bf16[16,2,16,16,512]{4,3,1,2,0:T(8,128)(2,1)}), bf16[16,2,16,16,512]{4,3,1,2,0:T(8,128)(2,1)}, u32[]{:S(2)}, u32[]{:S(2)}) %all-to-all-start.1) | async-done | bytes 8388640 | tf_op jit(solution)/shard_map/all_to_all | solution.py:17
  449.3 12.5 %reshape_reshape.3 = bf16[2,256,16,2,256]{4,3,2,0,1:T(2,128)(2,1)} reshape(bf16[2,16,16,16,512]{4,3,0,2,1:T(8,128)(2,1)} %bitcast.35) | data formatting | bytes 16777216 | tf_op jit(solution)/shard_map/reshape;reshape | solution.py:80
  461.8 21.3 %fusion.40 = bf16[2,16,256,512]{3,2,0,1:T(8,128)(2,1)} fusion(f32[16,256]{1,0:T(8,128)S(1)} %fusion.89, bf16[16,256,1,512]{3,1,2,0:T(8,128)(2,1)} %get-tuple-element.27, bf16[16,256,1,512]{3,1,2,0:T(8,128)(2,1)} %get-tuple-element.26, bf16[2,256,16,2,256]{4,3,2,0,1:T(2,128)(2,1)} %reshape_reshape.3), kind=kOutput, calls=%fused_computation.43 | convolution fusion | flops 4307550208 | bytes 25182208 | tf_op jit(solution)/shard_map/tspj,estpc->etcj/dot_general | solution.py:82
  483.1 13.0 %fusion.17 = bf16[16,2,256,256,2]{3,2,4,1,0:T(8,128)(2,1)} fusion(bf16[2,16,256,512]{3,2,0,1:T(8,128)(2,1)} %fusion.40, f32[16,256]{1,0:T(8,128)S(1)} %fusion.89, f32[16,256,512]{2,1,0:T(8,128)} %convert_element_type.68, bf16[16,256,1,512]{3,1,2,0:T(8,128)(2,1)} %get-tuple-element.27, bf16[16,256,1,512]{3,1,2,0:T(8,128)(2,1)} %get-tuple-element.26), kind=kOutput, calls=%fused_computation.26 | convolution fusion | flops 4332716032 | bytes 33570816 | tf_op jit(solution)/shard_map/tspj,etcj->etspc/dot_general | solution.py:91
  496.1 48.6 %fusion.95 = (bf16[2,16,16,512]{2,3,0,1:T(8,128)(2,1)}, bf16[2,16,16,512]{2,3,0,1:T(8,128)(2,1)}, bf16[2,16,16,512]{2,3,0,1:T(8,128)(2,1)}, bf16[2,16,16,512]{2,...) fusion(bf16[2,16,256,512]{2,3,0,1:T(8,128)(2,1)} %bitcast.215), kind=kLoop, calls=%fused_computation.141 | loop fusion | bytes 16777216 | tf_op jit(solution)/shard_map/split | solution.py:16
  544.7 3.5 copy.188
  548.2 3.5 copy.187
  551.7 3.5 copy.186
  555.2 3.5 copy.185
  558.7 3.5 copy.184
  562.2 3.5 copy.183
  565.7 4.4 copy.182
  570.1 4.4 copy.181
  574.5 4.4 copy.180
  579.0 4.4 copy.179
  583.4 4.4 copy.178
  587.9 4.5 copy.177
  592.3 4.5 copy.176
  596.8 4.5 copy.175
  601.2 4.5 copy.174
  605.7 4.5 copy.173
  610.2 1.2 bitcast_dynamic-update-slice_fusion.15
  611.3 1.1 bitcast_dynamic-update-slice_fusion.14
  612.4 1.1 bitcast_dynamic-update-slice_fusion.13
  613.5 1.1 bitcast_dynamic-update-slice_fusion.12
  614.6 1.1 bitcast_dynamic-update-slice_fusion.11
  615.6 1.1 bitcast_dynamic-update-slice_fusion.10
  616.7 1.1 bitcast_dynamic-update-slice_fusion.9
  617.8 1.1 bitcast_dynamic-update-slice_fusion.8
  619.3 218.8 %all_to_all.40 = bf16[16,2,16,16,512]{4,3,2,1,0:T(8,128)(2,1)} all-to-all(bf16[16,2,16,16,512]{4,3,2,1,0:T(8,128)(2,1)S(1)} %bitcast_dynamic-update-slice_fusion), channel_id=1, replica_groups=mesh['wave'=16,'lev'=2] {'wave'}, dimensions={0} | all-to-all | bytes 16777216 | tf_op jit(solution)/shard_map/all_to_all | solution.py:17
  838.1 8.5 copy.125
  846.6 17.0 %fusion.14 = bf16[16,2,512,256]{3,2,1,0:T(8,128)(2,1)} fusion(bf16[2,256,16,512]{3,2,1,0:T(8,128)(2,1)} %bitcast.220, bf16[16,256,256]{1,2,0:T(8,128)(2,1)S(1)} %copy-done.3), kind=kOutput, calls=%fused_computation.25 | convolution fusion | flops 2151677952 | bytes 18874368 | tf_op jit(solution)/shard_map/skt,etsq->eskq/dot_general | solution.py:98
  863.6 21.1 %copy.128 = bf16[2,16,256,2,256]{4,3,1,0,2:T(2,128)(2,1)} copy(bf16[2,16,256,2,256]{2,4,3,0,1:T(8,128)(2,1)} %bitcast.221) | data formatting | bytes 16777216 | tf_op jit(solution)/shard_map/reshape | solution.py:104
  884.7 7.2 all-to-all-start.3
  891.9 7.7 copy.140
  899.5 86.1 %all-to-all-done.3 = bf16[2,16,256,2,256]{4,3,1,0,2:T(2,128)(2,1)} async-done(((bf16[2,16,256,2,256]{4,3,1,0,2:T(2,128)(2,1)}), bf16[2,16,256,2,256]{4,3,1,0,2:T(2,128)(2,1)}, u32[]{:S(2)}, u32[]{:S(2)}) %all-to-all-start.3) | async-done | bytes 8388640 | tf_op jit(solution)/shard_map/all_to_all | solution.py:107
  985.6 13.6 %copy.129 = bf16[2,16,256,2,256]{4,2,3,1,0:T(8,128)(2,1)} copy(bf16[2,16,256,2,256]{4,3,1,0,2:T(2,128)(2,1)} %all-to-all-done.3) | data formatting | bytes 16777216 | tf_op jit(solution)/shard_map/all_to_all | solution.py:107
  999.2 12.1 %copy.130 = bf16[2,16,128,2,2,256]{2,5,4,3,1,0:T(8,128)(2,1)} copy(bf16[2,16,128,2,2,256]{5,2,4,3,1,0:T(8,128)(2,1)} %bitcast.224) | data formatting | bytes 16777216 | tf_op jit(solution)/shard_map/all_to_all | solution.py:107
  1011.3 11.5 %fusion.23 = f32[4,2,16,128,2,128]{3,5,4,2,1,0:T(8,128)} fusion(bf16[2,16,128,2,4,128]{2,5,4,3,1,0:T(8,128)(2,1)} %bitcast.216, bf16[4,4,128,128]{3,2,1,0:T(8,128)(2,1)S(1)} %copy-done.5), kind=kOutput, calls=%fused_computation.30 | convolution fusion | flops 1073741824 | bytes 25296896 | tf_op jit(solution)/shard_map/eskpal,alm->eskpam/dot_general | solution.py:43
  1022.8 11.5 %fusion.21 = f32[4,2,16,128,2,128]{3,5,4,2,1,0:T(8,128)} fusion(bf16[2,16,128,2,4,128]{2,5,4,3,1,0:T(8,128)(2,1)} %bitcast.217, bf16[4,4,128,128]{3,2,1,0:T(8,128)(2,1)S(1)} %copy-done.5), kind=kOutput, calls=%fused_computation.28 | convolution fusion | flops 1073741824 | bytes 25296896 | tf_op jit(solution)/shard_map/eskpal,alm->eskpam/dot_general | solution.py:43
  1034.3 11.5 %fusion.25 = f32[4,2,16,128,2,128]{3,5,4,2,1,0:T(8,128)} fusion(bf16[2,16,128,2,4,128]{2,5,4,3,1,0:T(8,128)(2,1)} %bitcast.218, bf16[4,4,128,128]{3,2,1,0:T(8,128)(2,1)S(1)} %copy-done.5), kind=kOutput, calls=%fused_computation.32 | convolution fusion | flops 1073741824 | bytes 25296896 | tf_op jit(solution)/shard_map/eskpal,alm->eskpam/dot_general | solution.py:43
  1045.8 23.0 %fusion.37 = bf16[2,16,128,2,4,128]{2,5,3,1,0,4:T(8,128)(2,1)} fusion(bf16[2,16,128,2,4,128]{2,5,4,3,1,0:T(8,128)(2,1)} %bitcast.219, pred[16,128]{1,0:T(8,128)(4,1)S(1)} %copy-done.14, f32[4,2,16,128,2,128]{3,5,4,2,1,0:T(8,128)} %fusion.21, pred[16,128]{1,0:T(8,128)(4,1)S(1)} %copy-done.16, f32[4,2,16,128,2,128]{3,5,4,2,1,0:T(8,128)} %fusion.23, ...), kind=kOutput, calls=%fused_computation.42 | convolution fusion | flops 1107296256 | bytes 67248128 | tf_op jit(solution)/shard_map/eskpal,alm->eskpam/dot_general | solution.py:43
  1068.8 10.4 copy.139
  1079.2 21.1 %copy.141 = bf16[2,16,128,2,512]{4,3,2,1,0:T(2,128)(2,1)} copy(bf16[2,16,128,2,512]{2,4,3,1,0:T(8,128)(2,1)} %bitcast.225) | data formatting | bytes 16777216
  (73 shorter events, 12.3 us)
Async XLA Ops:
  7.2 298.5 %copy-start = (f32[8,256]{1,0:T(8,128)S(1)}, f32[8,256]{1,0:T(8,128)}, u32[]{:S(2)}) copy-start(f32[8,256]{1,0:T(8,128)} %param.14) | copy-start | bytes 24580
  7.2 14.1 %copy-start.4 = (bf16[4,4,128,128]{3,2,1,0:T(8,128)(2,1)S(1)}, bf16[4,4,128,128]{3,2,1,0:T(8,128)(2,1)}, u32[]{:S(2)}) copy-start(bf16[4,4,128,128]{3,2,1,0:T(8,128)(2,1)} %param.11) | copy-start | bytes 1572868
  21.3 11.7 %copy-start.2 = (bf16[2,16,128,2,4,128]{5,4,3,2,1,0:T(4,128)(2,1)S(1)}, bf16[2,16,128,2,4,128]{5,4,3,2,1,0:T(4,128)(2,1)}, u32[]{:S(2)}) copy-start(bf16[2,16,128,2,4,128]{5,4,3,2,1,0:T(4,128)(2,1)} %reshape.278) | copy-start | bytes 25165828
  41.0 8.1 copy-start.17
  49.3 0.6 copy-start.9
  49.3 0.6 copy-start.11
  49.3 0.6 copy-start.13
  49.3 0.6 copy-start.15
  97.5 7.2 copy-start.8
  97.5 123.5 %all-to-all-start = ((bf16[2,16,128,2,512]{2,3,1,0,4:T(2,128)(2,1)}), bf16[2,16,128,2,512]{2,3,1,0,4:T(2,128)(2,1)}, u32[]{:S(2)}, u32[]{:S(2)}) async-start(bf16[2,16,128,2,512]{2,3,1,0,4:T(2,128)(2,1)} %copy.104), calls=%async_computation | async-start | bytes 16777216 | tf_op jit(solution)/shard_map/all_to_all | solution.py:65
  104.6 168.4 %all-gather.2.cloned.1.call-start = ((), (), s32[]{:S(2)}) async-start(), calls=%async_computation.4 | async-start | bytes 3145728 | tf_op jit(solution)/shard_map/all_gather | solution.py:72
  292.6 156.7 %all-to-all-start.1 = ((bf16[16,2,16,16,512]{4,3,1,2,0:T(8,128)(2,1)}), bf16[16,2,16,16,512]{4,3,1,2,0:T(8,128)(2,1)}, u32[]{:S(2)}, u32[]{:S(2)}) async-start(bf16[16,2,16,16,512]{4,3,1,2,0:T(8,128)(2,1)} %fusion.45), calls=%async_computation.1 | async-start | bytes 16777216 | tf_op jit(solution)/shard_map/all_to_all | solution.py:17
  298.8 6.8 copy-start.18
  298.8 6.9 copy-start.19
  610.1 8.7 copy-start.7
  610.1 8.8 copy-start.6
  838.1 8.5 copy-start.3
  884.7 100.9 %all-to-all-start.3 = ((bf16[2,16,256,2,256]{4,3,1,0,2:T(2,128)(2,1)}), bf16[2,16,256,2,256]{4,3,1,0,2:T(2,128)(2,1)}, u32[]{:S(2)}, u32[]{:S(2)}) async-start(bf16[2,16,256,2,256]{4,3,1,0,2:T(2,128)(2,1)} %copy.128), calls=%async_computation.3 | async-start | bytes 16777216 | tf_op jit(solution)/shard_map/all_to_all | solution.py:107
  999.2 12.1 %copy-start.5 = (bf16[4,4,128,128]{3,2,1,0:T(8,128)(2,1)S(1)}, bf16[4,4,128,128]{3,2,1,0:T(8,128)(2,1)}, u32[]{:S(2)}) copy-start(bf16[4,4,128,128]{3,2,1,0:T(8,128)(2,1)} %param.11) | copy-start | bytes 1572868
  1034.3 11.5 %copy-start.10 = (pred[16,128]{1,0:T(8,128)(4,1)S(1)}, pred[16,128]{1,0:T(8,128)(4,1)}, u32[]{:S(2)}) copy-start(pred[16,128]{1,0:T(8,128)(4,1)} %copy-done.9) | copy-start | bytes 6148
  1034.3 11.5 %copy-start.12 = (pred[16,128]{1,0:T(8,128)(4,1)S(1)}, pred[16,128]{1,0:T(8,128)(4,1)}, u32[]{:S(2)}) copy-start(pred[16,128]{1,0:T(8,128)(4,1)} %copy-done.11) | copy-start | bytes 6148
  1034.3 11.5 %copy-start.14 = (pred[16,128]{1,0:T(8,128)(4,1)S(1)}, pred[16,128]{1,0:T(8,128)(4,1)}, u32[]{:S(2)}) copy-start(pred[16,128]{1,0:T(8,128)(4,1)} %copy-done.13) | copy-start | bytes 6148
  1034.3 11.5 %copy-start.16 = (pred[16,128]{1,0:T(8,128)(4,1)S(1)}, pred[16,128]{1,0:T(8,128)(4,1)}, u32[]{:S(2)}) copy-start(pred[16,128]{1,0:T(8,128)(4,1)} %copy-done.15) | copy-start | bytes 6148
  1079.2 21.1 %copy-start.1 = (f32[8,256]{1,0:T(8,128)S(1)}, f32[8,256]{1,0:T(8,128)}, u32[]{:S(2)}) copy-start(f32[8,256]{1,0:T(8,128)} %param.14) | copy-start | bytes 24580
Sparse Core Ops, SparseCore 0:
  106.9 58.8 all-gather.1
